TPU v7x, 32 devices: a whole 2x2x4 slice. The times are simulated.
32 devices in a mesh: row: 4 (over x, core), col: 8 (over z, y).
Axes of the slice: x: 2, y: 2, z: 4, core: 2. Of those that a mesh axis runs over, the one named last changes fastest.
Arguments:
- pooled: bfloat16 [2048, 1152], P(('row', 'col')), may hold values from -32 to 32
- hidden: bfloat16 [2048, 4304], P(('row', 'col')), may hold values from -6 to 6
- text: bfloat16 [2048, 1152], P(('row', 'col')), may hold values from -12 to 12
- weight: float32 [1152, 4304], P('col', 'row'), may hold values from -0.09375 to 0.09375
- row_moment: float32 [1152], P('col'), may hold values from 1e-07 to 1e-05
- col_moment: float32 [4304], P('row'), may hold values from 1e-07 to 1e-05
- log_scale: float32 [], replicated, may hold values from 4.2 to 4.8
- bias: float32 [], replicated, may hold values from -16 to -12
Outputs:
- update: float32 [1152, 4304], P('col', 'row')
- new_row: float32 [1152], P('col')
- new_col: float32 [4304], P('row')
- loss: float32 [], replicated
All inputs are finite; a program needn't handle non-finite values.
Results may differ from a plain program's by a relative error of at most 0.004.
Values may be sent and summed in bfloat16 or wider, within the bound.
A program may use at most 128 MiB of HBM per device.

v0:
```python
import jax
import jax.numpy as jnp
from jax import lax
from jax.sharding import PartitionSpec as P

D = 1152
FF = 4304
EPSILON = 1e-06
DECAY_RATE = 0.8
CLIP_LEVEL = 1.0
FLOOR_VALUE = 1e-30


def over_row_index(positions, column, tokens, columns):
    return (positions // tokens * columns + column) * tokens + positions % tokens


def over_col_index(positions, row_place, tokens, columns):
    return row_place * columns * tokens + positions


def pair_tile(images, image_ids, texts, text_ids, logit_scale, bias, batch_total):
    logits = logit_scale * jnp.dot(images, texts.T, preferred_element_type=jnp.float32) + bias
    label_sign = jnp.where(
        image_ids[:, None] == text_ids[None, :], jnp.float32(1.0), jnp.float32(-1.0)
    )
    loss_sum = jnp.sum(jax.nn.softplus(-label_sign * logits))
    grad_logits = (-label_sign * jax.nn.sigmoid(-label_sign * logits) / batch_total).astype(
        jnp.bfloat16
    )
    return (loss_sum, logit_scale * jnp.dot(grad_logits, texts, preferred_element_type=jnp.float32))


def per_device(pooled, hidden, text, weight, row_moment, col_moment, log_scale, bias):
    rows_count = lax.axis_size("row")
    cols_count = lax.axis_size("col")
    row_place = lax.axis_index("row")
    col_place = lax.axis_index("col")
    tokens = pooled.shape[0]
    batch_total = tokens * rows_count * cols_count
    split_hidden = lax.all_to_all(hidden, "row", split_axis=1, concat_axis=0, tiled=True)
    hidden_cols = split_hidden.shape[1]
    weight_half = weight.astype(jnp.bfloat16)
    grouped = split_hidden.reshape(rows_count, tokens, hidden_cols)
    hidden_all = lax.all_gather(grouped, "col", axis=1, tiled=True).reshape(
        batch_total, hidden_cols
    )
    partial_proj = lax.dot_general(
        weight_half, hidden_all, (((1,), (1,)), ((), ())), preferred_element_type=jnp.float32
    )
    summed = lax.psum_scatter(partial_proj, "row", scatter_dimension=1, tiled=True)
    projected = lax.all_to_all(summed, "col", split_axis=1, concat_axis=0, tiled=True).T
    mixed_rows = pooled.astype(jnp.float32) + projected
    length = jnp.sqrt(jnp.sum(mixed_rows * mixed_rows, axis=1, keepdims=True) + EPSILON)
    image_unit = mixed_rows / length
    images = image_unit.astype(jnp.bfloat16)
    text_float = text.astype(jnp.float32)
    text_units = (
        text_float / jnp.sqrt(jnp.sum(text_float * text_float, axis=1, keepdims=True) + EPSILON)
    ).astype(jnp.bfloat16)
    logit_scale = jnp.exp(log_scale)
    image_rows = lax.all_gather(images, "row", axis=0, tiled=True)
    image_ids = over_row_index(
        jnp.arange(image_rows.shape[0], dtype=jnp.int32), col_place, tokens, cols_count
    )
    piece = lax.all_gather(text_units, "col", axis=0, tiled=True)
    text_ids = over_col_index(
        jnp.arange(piece.shape[0], dtype=jnp.int32), row_place, tokens, cols_count
    )
    loss_local, unit_part = pair_tile(
        image_rows, image_ids, piece, text_ids, logit_scale, bias, batch_total
    )
    unit_grad = lax.psum_scatter(unit_part, "row", scatter_dimension=0, tiled=True)
    mixed_grad = (
        (unit_grad - image_unit * jnp.sum(image_unit * unit_grad, axis=1, keepdims=True)) / length
    ).astype(jnp.bfloat16)
    grad_cols = lax.all_to_all(mixed_grad.T, "col", split_axis=0, concat_axis=1, tiled=True)
    gradient = jnp.dot(
        lax.all_gather(grad_cols, "row", axis=1, tiled=True),
        hidden_all,
        preferred_element_type=jnp.float32,
    )
    squared = gradient * gradient + FLOOR_VALUE
    row_sum = lax.psum(jnp.sum(squared, axis=1), "row")
    col_sum = lax.psum(jnp.sum(squared, axis=0), "col")
    new_row = DECAY_RATE * row_moment + (1.0 - DECAY_RATE) * row_sum / FF
    new_col = DECAY_RATE * col_moment + (1.0 - DECAY_RATE) * col_sum / D
    second = new_row[:, None] * new_col[None, :]
    raw_update = gradient / jnp.sqrt(second)
    loss_total = lax.psum(loss_local, ("row", "col"))
    update_total = lax.psum(jnp.sum(raw_update * raw_update), ("row", "col"))
    update_rms = jnp.sqrt(update_total / (D * FF))
    update = raw_update / jnp.maximum(1.0, update_rms / CLIP_LEVEL)
    loss = loss_total / batch_total
    return (update, new_row, new_col, loss)


def solution(mesh):
    return jax.shard_map(
        per_device,
        mesh=mesh,
        in_specs=(
            P(("row", "col"), None),
            P(("row", "col"), None),
            P(("row", "col"), None),
            P("col", "row"),
            P("col"),
            P("row"),
            P(),
            P(),
        ),
        out_specs=(P("col", "row"), P("col"), P("row"), P()),
        check_vma=False,
    )
```

profile of v0, /device:TPU:12, one launch (start us, length us, event | category | flops | bytes accessed | tf_op | source)
XLA Modules:
  0.0 324.7 jit_solution(10579943734243616240)
XLA Ops:
  7.2 1.5 all_to_all.40
  8.8 12.1 %all_to_all.54 = bf16[64,4,1076]{2,0,1:T(8,128)(2,1)S(1)} all-to-all(bf16[64,4,1076]{2,0,1:T(8,128)(2,1)S(1)} %copy.22), channel_id=1, replica_groups=mesh['row'=4,'col'=8] {'row'}, dimensions={1} | all-to-all | bytes 1101824 | tf_op jit(solution)/shard_map/all_to_all | solution.py:41
  20.9 1.3 copy.23
  22.2 78.1 %all-gather.3.cloned.1.call-done = bf16[4,512,1076]{2,0,1:T(4,128)(2,1)} async-done(((bf16[4,64,1076]{2,0,1:T(4,128)(2,1)}), bf16[4,512,1076]{2,0,1:T(4,128)(2,1)}) %all-gather.3.cloned.1.call-update) | async-done | bytes 4407312 | tf_op jit(solution)/shard_map/all_gather | solution.py:45
  100.3 10.4 %copy.24 = bf16[4,512,1076]{1,0,2:T(4,128)(2,1)} copy(bf16[4,512,1076]{2,0,1:T(4,128)(2,1)} %all-gather.3.cloned.1.call-done) | data formatting | bytes 8814592 | tf_op jit(solution)/shard_map/all_gather | solution.py:45
  110.7 3.9 %pad = bf16[1080,4,512]{2,1,0:T(4,128)(2,1)S(1)} pad(bf16[1076,4,512]{2,1,0:T(4,128)(2,1)} %bitcast.38, bf16[]{:T(256)} %constant.79), padding=0_4x0_0x0_0 | pad | bytes 8830978
  114.6 1.9 copy.31
  116.5 2.0 copy-done
  118.5 2.2 fusion.6
  122.6 23.8 %reduce-scatter.3.cloned.1.call-done = f32[144,512]{1,0:T(8,128)} async-done(((f32[144,2048]{1,0:T(8,128)}), f32[144,512]{1,0:T(8,128)}) %reduce-scatter.3.cloned.1.call-update) | async-done | bytes 294928 | tf_op jit(solution)/shard_map/reduce_scatter | solution.py:51
  146.4 2.0 copy.29
  148.3 6.1 %all-to-all-start.1 = ((f32[144,8,64]{0,2,1:T(8,128)}), f32[144,8,64]{0,2,1:T(8,128)S(1)}, u32[]{:S(2)}, u32[]{:S(2)}) async-start(f32[144,8,64]{0,2,1:T(8,128)} %bitcast.1), calls=%async_computation.2 | async-start | bytes 1048576 | tf_op jit(solution)/shard_map/all_to_all | solution.py:52
  155.8 14.4 %all-to-all-done.1 = f32[144,8,64]{0,2,1:T(8,128)S(1)} async-done(((f32[144,8,64]{0,2,1:T(8,128)}), f32[144,8,64]{0,2,1:T(8,128)S(1)}, u32[]{:S(2)}, u32[]{:S(2)}) %all-to-all-start.1) | async-done | bytes 294944 | tf_op jit(solution)/shard_map/all_to_all | solution.py:52
  171.0 7.1 %all_gather.13 = bf16[256,1152]{1,0:T(8,128)(2,1)S(1)} all-gather(bf16[64,1152]{1,0:T(8,128)(2,1)S(1)} %fusion.26), channel_id=1, replica_groups=mesh['row'=4,'col'=8] {'row'}, dimensions={0}, use_global_device_ids=true | all-gather | bytes 737280 | tf_op jit(solution)/shard_map/all_gather | solution.py:62
  178.1 12.6 %all-gather.5.cloned.1.call-done = bf16[512,1152]{1,0:T(8,128)(2,1)} async-done(((bf16[64,1152]{1,0:T(8,128)(2,1)}), bf16[512,1152]{1,0:T(8,128)(2,1)}) %all-gather.5.cloned.1.call-update) | async-done | bytes 1179664 | tf_op jit(solution)/shard_map/all_gather | solution.py:66
  190.6 2.9 fusion.5
  193.5 1.6 convolution_multiply_fusion
  195.1 26.1 %reduce-scatter.5.cloned.1.call-done = f32[64,1152]{1,0:T(8,128)} async-done(((f32[256,1152]{1,0:T(8,128)}), f32[64,1152]{1,0:T(8,128)}) %reduce-scatter.5.cloned.1.call-update) | async-done | bytes 294928 | tf_op jit(solution)/shard_map/reduce_scatter | solution.py:73
  223.9 12.6 %all_to_all.55 = bf16[8,144,64]{1,2,0:T(8,128)(2,1)S(1)} all-to-all(bf16[8,144,64]{1,2,0:T(8,128)(2,1)S(1)} %copy.27), channel_id=1, replica_groups=mesh['row'=4,'col'=8] {'col'}, dimensions={0} | all-to-all | bytes 294912 | tf_op jit(solution)/shard_map/all_to_all | solution.py:77
  236.6 6.7 %all_gather.15 = bf16[144,2048]{1,0:T(8,128)(2,1)S(1)} all-gather(bf16[144,512]{1,0:T(8,128)(2,1)S(1)} %copy.30), channel_id=1, replica_groups=mesh['row'=4,'col'=8] {'row'}, dimensions={1}, use_global_device_ids=true | all-gather | bytes 737280 | tf_op jit(solution)/shard_map/all_gather | solution.py:79
  243.3 4.1 %fusion.3 = (f32[144]{0:T(256)S(1)}, f32[1076]{0:T(1024)S(1)}, f32[144,1076]{1,0:T(8,128)S(1)}) fusion(bf16[144,2048]{1,0:T(8,128)(2,1)S(1)} %all_gather.15, bf16[2048,1076]{0,1:T(8,128)(2,1)} %bitcast.36), kind=kOutput, calls=%fused_computation.9 | convolution fusion | flops 635269184 | bytes 5621776 | tf_op jit(solution)/shard_map/dot_general | solution.py:78
  247.3 16.7 %psum.29 = f32[1076]{0:T(1024)S(1)} all-reduce(f32[1076]{0:T(1024)S(1)} %get-tuple-element.5), channel_id=1, replica_groups=mesh['row'=4,'col'=8] {'col'}, use_global_device_ids=true, to_apply=%region_8.9 | all-reduce | flops 1076 | bytes 8608 | tf_op jit(solution)/shard_map/psum | solution.py:85
  264.0 5.7 %psum.28 = f32[144]{0:T(256)S(1)} all-reduce(f32[144]{0:T(256)S(1)} %get-tuple-element.4), channel_id=1, replica_groups=mesh['row'=4,'col'=8] {'row'}, use_global_device_ids=true, to_apply=%region_6.7 | all-reduce | flops 144 | bytes 1152 | tf_op jit(solution)/shard_map/psum | solution.py:84
  270.7 44.0 %all-reduce = (f32[]{:T(128)}, f32[]{:T(128)}) all-reduce(f32[]{:T(128)} %multiply_reduce_fusion, f32[]{:T(128)} %get-tuple-element.9), channel_id=1, replica_groups=mesh['row'=4,'col'=8] {'row','col'}, use_global_device_ids=true, to_apply=%region_10.11 | all-reduce | flops 2 | bytes 16 | tf_op jit(solution)/shard_map/psum | solution.py:91
  (45 shorter events, 7.5 us)
Async XLA Ops:
  7.2 93.2 %all-gather.3.cloned.1.call-start = ((), (), s32[]{:S(2)}) async-start(), calls=%async_computation.5 | async-start | bytes 5308416 | tf_op jit(solution)/shard_map/all_gather | solution.py:45
  22.2 124.2 %reduce-scatter.3.cloned.1.call-start = ((), (), s32[]{:S(2)}) async-start(), calls=%async_computation.6 | async-start | bytes 1474560 | tf_op jit(solution)/shard_map/reduce_scatter | solution.py:51
  114.6 3.9 %copy-start.2 = (f32[144,1076]{1,0:T(8,128)S(1)}, f32[144,1076]{1,0:T(8,128)}, u32[]{:S(2)}) copy-start(f32[144,1076]{1,0:T(8,128)} %param.11) | copy-start | bytes 1859332
  116.5 2.0 copy-start
  120.8 0.9 copy-start.3
  120.8 69.8 %all-gather.5.cloned.1.call-start = ((), (), s32[]{:S(2)}) async-start(), calls=%async_computation.7 | async-start | bytes 1327104 | tf_op jit(solution)/shard_map/all_gather | solution.py:66
  148.3 21.8 %all-to-all-start.1 = ((f32[144,8,64]{0,2,1:T(8,128)}), f32[144,8,64]{0,2,1:T(8,128)S(1)}, u32[]{:S(2)}, u32[]{:S(2)}) async-start(f32[144,8,64]{0,2,1:T(8,128)} %bitcast.1), calls=%async_computation.2 | async-start | bytes 1048576 | tf_op jit(solution)/shard_map/all_to_all | solution.py:52
  154.4 16.3 %copy-start.1 = (bf16[64,1152]{1,0:T(8,128)(2,1)S(1)}, bf16[64,1152]{1,0:T(8,128)(2,1)}, u32[]{:S(2)}) copy-start(bf16[64,1152]{1,0:T(8,128)(2,1)} %param.8) | copy-start | bytes 442372
  154.4 66.8 %reduce-scatter.5.cloned.1.call-start = ((), (), s32[]{:S(2)}) async-start(), calls=%async_computation.8 | async-start | bytes 1474560 | tf_op jit(solution)/shard_map/reduce_scatter | solution.py:73
  190.6 2.9 copy-start.8
  243.3 26.4 %copy-start.6 = (f32[1076]{0:T(1024)S(1)}, f32[1076]{0:T(1024)}, u32[]{:S(2)}) copy-start(f32[1076]{0:T(1024)} %param.13) | copy-start | bytes 12916
  243.3 26.4 %copy-start.7 = (f32[144]{0:T(256)S(1)}, f32[144]{0:T(256)}, u32[]{:S(2)}) copy-start(f32[144]{0:T(256)} %param.12) | copy-start | bytes 1732
  269.7 47.3 %copy-start.4 = (f32[1076]{0:T(1024)}, f32[1076]{0:T(1024)S(1)}, u32[]{:S(2)}) copy-start(f32[1076]{0:T(1024)S(1)} %multiply_add_fusion.1) | copy-start | bytes 12916
  269.7 47.3 %copy-start.5 = (f32[144]{0:T(256)}, f32[144]{0:T(256)S(1)}, u32[]{:S(2)}) copy-start(f32[144]{0:T(256)S(1)} %multiply_add_fusion.2) | copy-start | bytes 1732
Sparse Core Ops, SparseCore 0:
  22.3 78.0 all-gather.2
  120.9 25.4 reduce-scatter.2
  148.6 41.9 all-gather.4
  195.3 25.9 reduce-scatter.4
where the time goes:
time: 326 us; the launch traced here: 325 us
  waiting for transfers between devices  155 us (48%)
  blocking collectives  105 us (32%)
  local copies, waits for them, and re-layouts  24.9 us (8%)
  between operations  17.8 us (5%)
  matrix products  10.8 us (3%)
  starting transfers between devices  6.18 us (2%)
  other arithmetic  5.36 us (2%)
    all_gather x1, waiting for transfers between devices, per_device(): lax.all_gather(grouped, 'col', axis=1, tiled=True)  78.1 us
    psum x1, blocking collectives, per_device(): update_total = lax.psum(jnp.sum(raw_update * raw_update), ('row', 'col'))  44 us
    reduce_scatter x1, waiting for transfers between devices, per_device(): lax.psum_scatter(unit_part, 'row', scatter_dimension=0, tiled=True)  26.1 us
    reduce_scatter x1, waiting for transfers between devices, per_device(): lax.psum_scatter(partial_proj, 'row', scatter_dimension=1, tiled=True)  23.8 us
    psum x1, blocking collectives, per_device(): col_sum = lax.psum(jnp.sum(squared, axis=0), 'col')  16.7 us
    all_to_all x1, waiting for transfers between devices, per_device(): lax.all_to_all(summed, 'col', split_axis=1, concat_axis=0, tiled=True)  14.4 us
    all_to_all x1, blocking collectives, per_device(): lax.all_to_all(mixed_grad.T, 'col', split_axis=0, concat_axis=1, tiled=True)  12.6 us
    all_gather x1, waiting for transfers between devices, per_device(): piece = lax.all_gather(text_units, 'col', axis=0, tiled=True)  12.6 us
  transfers between devices with their start and end apart: 5, of which 5 were waited for; matrix products, arithmetic and copies ran while one was open for 1% of the time, Pallas kernels for 0%

commit v1 on v0

--- a/solution.py
+++ b/solution.py
@@ -42,7 +42,7 @@
     hidden_cols = split_hidden.shape[1]
     weight_half = weight.astype(jnp.bfloat16)
     grouped = split_hidden.reshape(rows_count, tokens, hidden_cols)
-    hidden_all = lax.all_gather(grouped, "col", axis=1, tiled=True).reshape(
+    hidden_all = jnp.concatenate(lax.all_gather(grouped, "col"), axis=1).reshape(
         batch_total, hidden_cols
     )
     partial_proj = lax.dot_general(

time: 326 us -> 311 us (0.954)
  local copies, waits for them, and re-layouts: 24.9 us -> 10.4 us
    all_gather x1 -> x0, local copies, waits for them, and re-layouts: 10.4 us -> none  [per_device(): lax.all_gather(grouped, 'col', axis=1, tiled=True)]
    unnamed x20 -> x18, local copies, waits for them, and re-layouts: 8.66 us -> 2.98 us
where the time goes in v1:
time: 311 us
  waiting for transfers between devices  155 us (50%)
  blocking collectives  105 us (34%)
  between operations  17.8 us (6%)
  matrix products  10.7 us (3%)
  local copies, waits for them, and re-layouts  10.4 us (3%)
  starting transfers between devices  6.15 us (2%)
  other arithmetic  5.35 us (2%)
    all_gather x1, waiting for transfers between devices, per_device(): lax.all_gather(grouped, 'col')  78.1 us
    psum x1, blocking collectives, per_device(): update_total = lax.psum(jnp.sum(raw_update * raw_update), ('row', 'col'))  44 us
    reduce_scatter x1, waiting for transfers between devices, per_device(): lax.psum_scatter(unit_part, 'row', scatter_dimension=0, tiled=True)  26.1 us
    reduce_scatter x1, waiting for transfers between devices, per_device(): lax.psum_scatter(partial_proj, 'row', scatter_dimension=1, tiled=True)  23.8 us
    psum x1, blocking collectives, per_device(): col_sum = lax.psum(jnp.sum(squared, axis=0), 'col')  16.7 us
    all_to_all x1, waiting for transfers between devices, per_device(): lax.all_to_all(summed, 'col', split_axis=1, concat_axis=0, tiled=True)  14.4 us
    all_to_all x1, blocking collectives, per_device(): lax.all_to_all(hidden, 'row', split_axis=1, concat_axis=0, tiled=True)  12.6 us
    all_to_all x1, blocking collectives, per_device(): lax.all_to_all(mixed_grad.T, 'col', split_axis=0, concat_axis=1, tiled=True)  12.6 us
  transfers between devices with their start and end apart: 5, of which 5 were waited for; matrix products, arithmetic and copies ran while one was open for 1% of the time, Pallas kernels for 0%

profile of v1, /device:TPU:12, one launch (start us, length us, event | category | flops | bytes accessed | tf_op | source)
XLA Modules:
  0.0 310.7 jit_solution(11505016949737498635)
XLA Ops:
  7.2 1.5 all_to_all.40
  8.8 12.6 %all_to_all.54 = bf16[64,4,1076]{2,0,1:T(8,128)(2,1)} all-to-all(bf16[64,4,1076]{2,0,1:T(8,128)(2,1)S(1)} %copy.22), channel_id=1, replica_groups=mesh['row'=4,'col'=8] {'row'}, dimensions={1} | all-to-all | bytes 1101824 | tf_op jit(solution)/shard_map/all_to_all | solution.py:41
  21.5 78.1 %all-gather.6.cloned.1.call-done = bf16[32,64,1076]{2,1,0:T(8,128)(2,1)} async-done(((bf16[4,64,1076]{2,1,0:T(8,128)(2,1)}), bf16[32,64,1076]{2,1,0:T(8,128)(2,1)}) %all-gather.6.cloned.1.call-update) | async-done | bytes 4407312 | tf_op jit(solution)/shard_map/all_gather | solution.py:45
  99.6 2.8 copy.23
  102.5 2.1 copy-done
  104.6 2.7 fusion.6
  109.2 23.8 %reduce-scatter.3.cloned.1.call-done = f32[144,512]{1,0:T(8,128)} async-done(((f32[144,2048]{1,0:T(8,128)}), f32[144,512]{1,0:T(8,128)}) %reduce-scatter.3.cloned.1.call-update) | async-done | bytes 294928 | tf_op jit(solution)/shard_map/reduce_scatter | solution.py:51
  132.9 2.0 copy.28
  134.9 6.0 %all-to-all-start.1 = ((f32[144,8,64]{0,2,1:T(8,128)}), f32[144,8,64]{0,2,1:T(8,128)S(1)}, u32[]{:S(2)}, u32[]{:S(2)}) async-start(f32[144,8,64]{0,2,1:T(8,128)} %bitcast.4), calls=%async_computation.2 | async-start | bytes 1048576 | tf_op jit(solution)/shard_map/all_to_all | solution.py:52
  142.3 14.4 %all-to-all-done.1 = f32[144,8,64]{0,2,1:T(8,128)S(1)} async-done(((f32[144,8,64]{0,2,1:T(8,128)}), f32[144,8,64]{0,2,1:T(8,128)S(1)}, u32[]{:S(2)}, u32[]{:S(2)}) %all-to-all-start.1) | async-done | bytes 294944 | tf_op jit(solution)/shard_map/all_to_all | solution.py:52
  157.5 7.1 %all_gather.13 = bf16[256,1152]{1,0:T(8,128)(2,1)S(1)} all-gather(bf16[64,1152]{1,0:T(8,128)(2,1)S(1)} %fusion.26), channel_id=1, replica_groups=mesh['row'=4,'col'=8] {'row'}, dimensions={0}, use_global_device_ids=true | all-gather | bytes 737280 | tf_op jit(solution)/shard_map/all_gather | solution.py:62
  164.6 12.6 %all-gather.4.cloned.1.call-done = bf16[512,1152]{1,0:T(8,128)(2,1)} async-done(((bf16[64,1152]{1,0:T(8,128)(2,1)}), bf16[512,1152]{1,0:T(8,128)(2,1)}) %all-gather.4.cloned.1.call-update) | async-done | bytes 1179664 | tf_op jit(solution)/shard_map/all_gather | solution.py:66
  177.2 2.9 fusion.5
  180.0 1.7 convolution_multiply_fusion
  181.7 26.1 %reduce-scatter.5.cloned.1.call-done = f32[64,1152]{1,0:T(8,128)} async-done(((f32[256,1152]{1,0:T(8,128)}), f32[64,1152]{1,0:T(8,128)}) %reduce-scatter.5.cloned.1.call-update) | async-done | bytes 294928 | tf_op jit(solution)/shard_map/reduce_scatter | solution.py:73
  207.8 1.2 multiply_reduce_fusion.1
  209.0 1.1 fusion.16
  210.5 12.6 %all_to_all.55 = bf16[8,144,64]{1,2,0:T(8,128)(2,1)S(1)} all-to-all(bf16[8,144,64]{1,2,0:T(8,128)(2,1)S(1)} %copy.26), channel_id=1, replica_groups=mesh['row'=4,'col'=8] {'col'}, dimensions={0} | all-to-all | bytes 294912 | tf_op jit(solution)/shard_map/all_to_all | solution.py:77
  223.2 6.7 %all_gather.15 = bf16[144,2048]{1,0:T(8,128)(2,1)S(1)} all-gather(bf16[144,512]{1,0:T(8,128)(2,1)S(1)} %copy.29), channel_id=1, replica_groups=mesh['row'=4,'col'=8] {'row'}, dimensions={1}, use_global_device_ids=true | all-gather | bytes 737280 | tf_op jit(solution)/shard_map/all_gather | solution.py:79
  229.9 3.5 %fusion.3 = (f32[144]{0:T(256)S(1)}, f32[1076]{0:T(1024)S(1)}, f32[144,1076]{1,0:T(8,128)S(1)}) fusion(bf16[144,2048]{1,0:T(8,128)(2,1)S(1)} %all_gather.15, bf16[2048,1076]{1,0:T(8,128)(2,1)} %bitcast.35), kind=kOutput, calls=%fused_computation.9 | convolution fusion | flops 635269184 | bytes 5621776 | tf_op jit(solution)/shard_map/dot_general | solution.py:78
  233.4 16.7 %psum.29 = f32[1076]{0:T(1024)S(1)} all-reduce(f32[1076]{0:T(1024)S(1)} %get-tuple-element.5), channel_id=1, replica_groups=mesh['row'=4,'col'=8] {'col'}, use_global_device_ids=true, to_apply=%region_8.9 | all-reduce | flops 1076 | bytes 8608 | tf_op jit(solution)/shard_map/psum | solution.py:85
  250.0 5.7 %psum.28 = f32[144]{0:T(256)S(1)} all-reduce(f32[144]{0:T(256)S(1)} %get-tuple-element.4), channel_id=1, replica_groups=mesh['row'=4,'col'=8] {'row'}, use_global_device_ids=true, to_apply=%region_6.7 | all-reduce | flops 144 | bytes 1152 | tf_op jit(solution)/shard_map/psum | solution.py:84
  256.7 44.0 %all-reduce = (f32[]{:T(128)}, f32[]{:T(128)}) all-reduce(f32[]{:T(128)} %multiply_reduce_fusion, f32[]{:T(128)} %get-tuple-element.9), channel_id=1, replica_groups=mesh['row'=4,'col'=8] {'row','col'}, use_global_device_ids=true, to_apply=%region_10.11 | all-reduce | flops 2 | bytes 16 | tf_op jit(solution)/shard_map/psum | solution.py:91
  301.4 1.0 fusion.4
  (42 shorter events, 4.3 us)
Async XLA Ops:
  7.2 92.5 %all-gather.6.cloned.1.call-start = ((), (), s32[]{:S(2)}) async-start(), calls=%async_computation.8 | async-start | bytes 5308416 | tf_op jit(solution)/shard_map/all_gather | solution.py:45
  21.4 111.5 %reduce-scatter.3.cloned.1.call-start = ((), (), s32[]{:S(2)}) async-start(), calls=%async_computation.5 | async-start | bytes 1474560 | tf_op jit(solution)/shard_map/reduce_scatter | solution.py:51
  99.6 5.0 %copy-start.2 = (f32[144,1076]{1,0:T(8,128)S(1)}, f32[144,1076]{1,0:T(8,128)}, u32[]{:S(2)}) copy-start(f32[144,1076]{1,0:T(8,128)} %param.11) | copy-start | bytes 1859332
  102.5 2.1 copy-start
  107.3 0.9 copy-start.3
  107.3 69.8 %all-gather.4.cloned.1.call-start = ((), (), s32[]{:S(2)}) async-start(), calls=%async_computation.6 | async-start | bytes 1327104 | tf_op jit(solution)/shard_map/all_gather | solution.py:66
  134.9 21.8 %all-to-all-start.1 = ((f32[144,8,64]{0,2,1:T(8,128)}), f32[144,8,64]{0,2,1:T(8,128)S(1)}, u32[]{:S(2)}, u32[]{:S(2)}) async-start(f32[144,8,64]{0,2,1:T(8,128)} %bitcast.4), calls=%async_computation.2 | async-start | bytes 1048576 | tf_op jit(solution)/shard_map/all_to_all | solution.py:52
  140.9 16.3 %copy-start.1 = (bf16[64,1152]{1,0:T(8,128)(2,1)S(1)}, bf16[64,1152]{1,0:T(8,128)(2,1)}, u32[]{:S(2)}) copy-start(bf16[64,1152]{1,0:T(8,128)(2,1)} %param.8) | copy-start | bytes 442372
  140.9 66.9 %reduce-scatter.5.cloned.1.call-start = ((), (), s32[]{:S(2)}) async-start(), calls=%async_computation.7 | async-start | bytes 1474560 | tf_op jit(solution)/shard_map/reduce_scatter | solution.py:73
  177.2 2.9 copy-start.8
  229.9 25.8 %copy-start.6 = (f32[1076]{0:T(1024)S(1)}, f32[1076]{0:T(1024)}, u32[]{:S(2)}) copy-start(f32[1076]{0:T(1024)} %param.13) | copy-start | bytes 12916
  229.9 25.8 %copy-start.7 = (f32[144]{0:T(256)S(1)}, f32[144]{0:T(256)}, u32[]{:S(2)}) copy-start(f32[144]{0:T(256)} %param.12) | copy-start | bytes 1732
  255.7 47.3 %copy-start.4 = (f32[1076]{0:T(1024)}, f32[1076]{0:T(1024)S(1)}, u32[]{:S(2)}) copy-start(f32[1076]{0:T(1024)S(1)} %multiply_add_fusion.1) | copy-start | bytes 12916
  255.7 47.3 %copy-start.5 = (f32[144]{0:T(256)}, f32[144]{0:T(256)S(1)}, u32[]{:S(2)}) copy-start(f32[144]{0:T(256)S(1)} %multiply_add_fusion.2) | copy-start | bytes 1732
Sparse Core Ops, SparseCore 0:
  21.6 78.0 all-gather.5
  107.5 25.4 reduce-scatter.2
  135.1 41.9 all-gather.3
  181.9 25.9 reduce-scatter.4
